TPU v7x, 32 devices: a whole 2x2x4 slice. The times are simulated.
32 devices in a mesh: view: 4 (over x, core), pencil: 8 (over z, y).
Axes of the slice: x: 2, y: 2, z: 4, core: 2. Of those that a mesh axis runs over, the one named last changes fastest.
Arguments:
- recorded: float32 [4, 256, 256, 256], P('view', 'pencil'), may hold values from 0.5 to 4
- spectral_weight: float32 [4, 256, 256, 256], P('view', None, 'pencil'), may hold values from 0.05 to 1
- psf_taps: float32 [4, 3, 9], replicated, may hold values from 0.1 to 1
Outputs:
- joined_volume: float32 [256, 256, 256], P('pencil', 'view')
- estimate: float32 [256, 256, 256], P('pencil', 'view')
All inputs are finite; a program needn't handle non-finite values.
Results may differ from a plain program's by a relative error of at most 0.00029.
Values sent between devices are 32-bit elements; how exact they have to be, the bound alone decides.
A program may use at most 192 MiB of HBM per device.

v0:
```python
import math

import jax
import jax.numpy as jnp
from jax import lax
from jax.sharding import PartitionSpec as P

NZ = 256
NY = 256
NX = 256
ITERS = 2


def padded_2(shard, sides, width):
    for axis, dim in sides:
        devices, length = (lax.axis_size(axis), shard.shape[dim])
        up = [(i, (i + 1) % devices) for i in range(devices - 1)]
        down = [(j, i) for i, j in up]
        last = lax.slice_in_dim(shard, length - width, length, axis=dim)
        leading = lax.slice_in_dim(shard, 0, width, axis=dim)
        before = lax.ppermute(last, axis, up)
        after = lax.ppermute(leading, axis, down)
        shard = jnp.concatenate([before, shard, after], axis=dim)
    return shard


def tables(length):
    positions = jnp.arange(length, dtype=jnp.int32)
    product = positions[:, None] * positions[None, :] % length
    phases = product.astype(jnp.float32) * (2.0 * math.pi / length)
    return (jnp.cos(phases), jnp.sin(phases))


def mix(form, left, right):
    return jnp.einsum(form, left, right, precision=lax.Precision.HIGHEST)


def depth_forward(pieces):
    real_part, imag_part = pieces
    cosine, sine_part = tables(real_part.shape[0])
    out_real = mix("zyx,zk->kyx", real_part, cosine) + mix("zyx,zk->kyx", imag_part, sine_part)
    out_imag = mix("zyx,zk->kyx", imag_part, cosine) - mix("zyx,zk->kyx", real_part, sine_part)
    return (out_real, out_imag)


def depth_inverse(real_part, imag_part):
    cosine, sine_part = tables(real_part.shape[0])
    out_real = mix("kyx,kz->zyx", real_part, cosine) - mix("kyx,kz->zyx", imag_part, sine_part)
    out_imag = mix("kyx,kz->zyx", real_part, sine_part) + mix("kyx,kz->zyx", imag_part, cosine)
    return (out_real, out_imag)


def rows_inverse(pieces):
    real_part, imag_part = pieces
    cosine, sine_part = tables(real_part.shape[1])
    out_real = mix("zkx,ky->zyx", real_part, cosine) - mix("zkx,ky->zyx", imag_part, sine_part)
    out_imag = mix("zkx,ky->zyx", real_part, sine_part) + mix("zkx,ky->zyx", imag_part, cosine)
    return (out_real, out_imag)


def columns_inverse(real_part, imag_part):
    cosine, sine_part = tables(real_part.shape[2])
    total = mix("zyk,kx->zyx", real_part, cosine) - mix("zyk,kx->zyx", imag_part, sine_part)
    return total / float(NZ * NY * NX)


def valid_conv(padded, column, axis_dim, length):
    running = column[0] * lax.slice_in_dim(padded, 0, length, axis=axis_dim)
    for offset in range(1, column.shape[0]):
        running = running + column[offset] * lax.slice_in_dim(
            padded, offset, offset + length, axis=axis_dim
        )
    return running


def padded_conv(field, column, axis_dim, margin):
    padding = [(0, 0)] * field.ndim
    padding[axis_dim] = (margin, margin)
    return valid_conv(jnp.pad(field, padding), column, axis_dim, field.shape[axis_dim])


def blur_views(padded, tap_rows, depth, rows_count, margin):
    field = valid_conv(padded, tap_rows[0], 1, depth)
    field = valid_conv(field, tap_rows[1], 2, rows_count)
    return padded_conv(field, tap_rows[2], 3, margin)


def body(recorded, spectral_weight, psf_taps):
    view_count = lax.axis_size("view")
    view_index = lax.axis_index("view")
    slab = recorded[0]
    cos_x, sin_x = tables(slab.shape[2])
    cos_y, sin_y = tables(slab.shape[1])
    first_real = mix("zyx,xk->zyk", slab, cos_x)
    first_imag = -mix("zyx,xk->zyk", slab, sin_x)
    second_real = mix("zyx,yk->zkx", first_real, cos_y) + mix("zyx,yk->zkx", first_imag, sin_y)
    second_imag = mix("zyx,yk->zkx", first_imag, cos_y) - mix("zyx,yk->zkx", first_real, sin_y)
    spec_real, spec_imag = depth_forward(
        (
            lax.all_to_all(second_real, "pencil", split_axis=1, concat_axis=0, tiled=True),
            lax.all_to_all(second_imag, "pencil", split_axis=1, concat_axis=0, tiled=True),
        )
    )
    weights = spectral_weight[0]
    weighted_real = spec_real * weights
    weighted_imag = spec_imag * weights
    quarter = slab.shape[1] // view_count
    start = view_index * quarter
    summed_real, summed_imag = lax.psum((weighted_real, weighted_imag), "view")
    inv_real, inv_imag = depth_inverse(summed_real, summed_imag)
    rows_real, rows_imag = rows_inverse(
        (
            lax.all_to_all(inv_real, "pencil", split_axis=0, concat_axis=1, tiled=True),
            lax.all_to_all(inv_imag, "pencil", split_axis=0, concat_axis=1, tiled=True),
        )
    )
    joined_full = columns_inverse(rows_real, rows_imag)
    joined_volume = lax.dynamic_slice_in_dim(joined_full, start, quarter, 1)
    kernels = psf_taps / jnp.sum(psf_taps, axis=-1, keepdims=True)
    margin = kernels.shape[-1] // 2
    stacked = lax.all_to_all(recorded, "view", split_axis=2, concat_axis=0, tiled=True)
    tap_rows = jnp.transpose(kernels, (1, 2, 0))[:, :, :, None, None, None]
    back_rows = tap_rows[:, ::-1]
    local = 0.1 + jax.nn.softplus(joined_volume)
    depth = local.shape[0]
    for repeat in range(ITERS):
        padded = padded_2(local, (("view", 1), ("pencil", 0)), margin)
        blurred = blur_views(padded[None], tap_rows, depth, quarter, margin)
        ratio = stacked / blurred
        padded_ratio = padded_2(ratio, (("view", 2), ("pencil", 1)), margin)
        correction = blur_views(padded_ratio, back_rows, depth, quarter, margin)
        local = local * jnp.sum(correction, axis=0) / view_count
    return (joined_volume, local)


def solution(mesh):
    return jax.shard_map(
        body,
        mesh=mesh,
        in_specs=(P("view", "pencil", None, None), P("view", None, "pencil", None), P()),
        out_specs=(P("pencil", "view", None), P("pencil", "view", None)),
        check_vma=False,
    )
```

profile of v0, /device:TPU:25, one launch (start us, length us, event | category | flops | bytes accessed | tf_op | source)
XLA Modules:
  0.0 1960.9 jit_solution(9329688927747642899)
XLA Ops:
  7.2 19.4 fusion.127
  59.1 18.3 add_bitcast_fusion
  91.5 18.3 fusion.119
  109.7 18.0 subtract_bitcast_fusion
  139.2 134.6 %all-to-all-done = f32[32,256,256]{2,0,1:T(8,128)} async-done(((f32[32,256,256]{2,0,1:T(8,128)}), f32[32,256,256]{2,0,1:T(8,128)}, u32[]{:S(2)}, u32[]{:S(2)}) %all-to-all-start) | async-done | bytes 8388640 | tf_op jit(solution)/shard_map/all_to_all | solution.py:100
  287.0 174.1 %all-to-all-done.1 = f32[32,256,256]{2,0,1:T(8,128)} async-done(((f32[32,256,256]{2,0,1:T(8,128)}), f32[32,256,256]{2,0,1:T(8,128)}, u32[]{:S(2)}, u32[]{:S(2)}) %all-to-all-start.1) | async-done | bytes 8388640 | tf_op jit(solution)/shard_map/all_to_all | solution.py:101
  495.2 20.9 %bitcast_multiply_fusion = f32[256,32,256]{2,0,1:T(8,128)} fusion(f32[256,32,256]{2,0,1:T(8,128)} %fusion.167, f32[1,256,32,256]{3,2,1,0:T(8,128)} %param.4, f32[256,32,256]{2,0,1:T(8,128)S(1)} %bitcast.175), kind=kOutput, calls=%fused_computation.211 | convolution fusion | flops 6447562752 | bytes 33554432 | tf_op jit(solution)/shard_map/zyx,zk->kyx/dot_general | solution.py:35
  516.1 24.1 %bitcast_multiply_fusion.1 = f32[256,32,256]{2,0,1:T(8,128)} fusion(f32[256,32,256]{2,0,1:T(8,128)} %fusion.172, f32[1,256,32,256]{3,2,1,0:T(8,128)} %param.4, f32[256,32,256]{2,0,1:T(8,128)} %bitcast.177), kind=kOutput, calls=%fused_computation.212 | convolution fusion | flops 6447562752 | bytes 33554432 | tf_op jit(solution)/shard_map/zyx,zk->kyx/dot_general | solution.py:35
  540.2 288.2 %all-reduce.7.cloned.1.call-done = (f32[256,32,256]{2,0,1:T(8,128)}, f32[256,32,256]{2,0,1:T(8,128)}) async-done(((f32[256,32,256]{2,0,1:T(8,128)}, f32[256,32,256]{2,0,1:T(8,128)}), (f32[256,32,256]{2,0,1:T(8,128)}, f32[256,32,256]{2,0,1:T(8,128)})) %all-reduce.7.cloned.1.call-update) | async-done | bytes 16777232 | tf_op jit(solution)/shard_map/psum | solution.py:109
  902.9 149.6 %all-to-all-done.3 = f32[256,32,256]{2,1,0:T(8,128)} async-done(((f32[256,32,256]{2,1,0:T(8,128)}), f32[256,32,256]{2,1,0:T(8,128)}, u32[]{:S(2)}, u32[]{:S(2)}) %all-to-all-start.3) | async-done | bytes 8388640 | tf_op jit(solution)/shard_map/all_to_all | solution.py:114
  1096.6 143.0 %all-to-all-done.2 = f32[256,32,256]{2,1,0:T(8,128)} async-done(((f32[256,32,256]{2,1,0:T(8,128)}), f32[256,32,256]{2,1,0:T(8,128)}, u32[]{:S(2)}, u32[]{:S(2)}) %all-to-all-start.2) | async-done | bytes 8388640 | tf_op jit(solution)/shard_map/all_to_all | solution.py:113
  1307.4 30.3 %collective-permute-done = f32[32,4,256]{2,1,0:T(4,128)S(1)} collective-permute-done((f32[32,4,256]{2,1,0:T(4,128)S(1)}, f32[32,4,256]{2,1,0:T(4,128)S(1)}, u32[]{:S(2)}, u32[]{:S(2)}) %collective-permute-start) | collective-permute-done | bytes 131104 | tf_op jit(solution)/shard_map/ppermute | solution.py:21
  1384.1 45.1 %fusion.26 = f32[4,32,64,256]{3,1,2,0:T(8,128)} fusion(f32[4,32,64,256]{3,1,2,0:T(8,128)} %bitcast.45, f32[4,32,64,256]{3,1,2,0:T(8,128)} %fusion.107, f32[4]{0:T(128)S(1)} %get-tuple-element.3, f32[4]{0:T(128)S(1)} %get-tuple-element.4, f32[4]{0:T(128)S(1)} %get-tuple-element.5, f32[4]{0:T(128)S(1)} %get-tuple-element.6, f32[4]{0:T(128)S(1)} %get-tuple-element.7, ...), kind=kLoop, calls=%fused_computation.82 | loop fusion | flops 37748736 | bytes 25165968 | tf_op jit(solution)/shard_map/div | solution.py:129
  1462.6 18.2 collective-permute-done.6
  1480.8 25.4 %collective-permute-done.7 = f32[4,4,72,256]{3,1,2,0:T(4,128)S(1)} collective-permute-done((f32[4,4,72,256]{3,1,2,0:T(4,128)S(1)}, f32[4,4,72,256]{3,1,2,0:T(4,128)S(1)}, u32[]{:S(2)}, u32[]{:S(2)}) %collective-permute-start.7) | collective-permute-done | bytes 1179680 | tf_op jit(solution)/shard_map/ppermute | solution.py:22
  1522.7 41.0 %fusion.9 = f32[4,32,72,256]{3,1,2,0:T(8,128)} fusion(f32[4,36,72,256]{3,1,2,0:T(8,128)} %get-tuple-element.38, f32[4,36,72,256]{3,1,2,0:T(8,128)} %get-tuple-element.37, f32[4]{0:T(128)S(1)} %get-tuple-element.17, f32[4]{0:T(128)S(1)} %get-tuple-element.18, f32[4]{0:T(128)S(1)} %get-tuple-element.19, f32[4]{0:T(128)S(1)} %get-tuple-element.20, ...), kind=kLoop, calls=%fused_computation.54 | loop fusion | flops 44826624 | bytes 94371984 | tf_op jit(solution)/shard_map/add | solution.py:70
  1563.7 29.6 %fusion.99 = f32[4,32,64,256]{3,1,2,0:T(8,128)} fusion(f32[4,32,72,256]{3,1,2,0:T(8,128)} %fusion.9, f32[4]{0:T(128)S(1)} %get-tuple-element.10, f32[4]{0:T(128)S(1)} %get-tuple-element.11, f32[4]{0:T(128)S(1)} %get-tuple-element.12, f32[4]{0:T(128)S(1)} %get-tuple-element.13, f32[4]{0:T(128)S(1)} %get-tuple-element.14, f32[4]{0:T(128)S(1)} %get-tuple-element.15, ...), kind=kLoop, calls=%fused_computation.174 | loop fusion | flops 35651584 | bytes 83886224 | tf_op jit(solution)/shard_map/add | solution.py:70
  1593.3 42.4 %fusion.134 = f32[32,64,256]{2,0,1:T(8,128)} fusion(f32[4,32,64,256]{3,1,2,0:T(8,128)} %fusion.99, f32[4]{0:T(128)S(1)} %get-tuple-element.3, f32[4]{0:T(128)S(1)} %get-tuple-element.4, f32[4]{0:T(128)S(1)} %get-tuple-element.5, f32[4]{0:T(128)S(1)} %get-tuple-element.6, f32[4]{0:T(128)S(1)} %get-tuple-element.7, f32[4]{0:T(128)S(1)} %get-tuple-element.8, ...), kind=kLoop, calls=%fused_computation.230 | loop fusion | flops 37224448 | bytes 10485904 | tf_op jit(solution)/shard_map/reduce_sum | solution.py:132
  1700.1 45.1 %fusion.59 = f32[4,32,64,256]{3,1,2,0:T(8,128)} fusion(f32[4,32,64,256]{3,1,2,0:T(8,128)} %bitcast.45, f32[4,32,64,256]{3,1,2,0:T(8,128)} %fusion.91, f32[4]{0:T(128)S(1)} %get-tuple-element.3, f32[4]{0:T(128)S(1)} %get-tuple-element.4, f32[4]{0:T(128)S(1)} %get-tuple-element.5, f32[4]{0:T(128)S(1)} %get-tuple-element.6, f32[4]{0:T(128)S(1)} %get-tuple-element.7, ...), kind=kLoop, calls=%fused_computation.115 | loop fusion | flops 37748736 | bytes 25165968 | tf_op jit(solution)/shard_map/div | solution.py:129
  1776.8 18.7 collective-permute-done.14
  1795.5 25.4 %collective-permute-done.15 = f32[4,4,72,256]{3,1,2,0:T(4,128)S(1)} collective-permute-done((f32[4,4,72,256]{3,1,2,0:T(4,128)S(1)}, f32[4,4,72,256]{3,1,2,0:T(4,128)S(1)}, u32[]{:S(2)}, u32[]{:S(2)}) %collective-permute-start.15) | collective-permute-done | bytes 1179680 | tf_op jit(solution)/shard_map/ppermute | solution.py:22
  1837.4 41.0 %fusion.1 = f32[4,32,72,256]{3,1,2,0:T(8,128)} fusion(f32[4,36,72,256]{3,1,2,0:T(8,128)} %get-tuple-element.34, f32[4,36,72,256]{3,1,2,0:T(8,128)} %get-tuple-element.33, f32[4]{0:T(128)S(1)} %get-tuple-element.17, f32[4]{0:T(128)S(1)} %get-tuple-element.18, f32[4]{0:T(128)S(1)} %get-tuple-element.19, f32[4]{0:T(128)S(1)} %get-tuple-element.20, ...), kind=kLoop, calls=%fused_computation.38 | loop fusion | flops 44826624 | bytes 94371984 | tf_op jit(solution)/shard_map/add | solution.py:70
  1878.4 29.6 %fusion.83 = f32[4,32,64,256]{3,1,2,0:T(8,128)} fusion(f32[4,32,72,256]{3,1,2,0:T(8,128)} %fusion.1, f32[4]{0:T(128)S(1)} %get-tuple-element.10, f32[4]{0:T(128)S(1)} %get-tuple-element.11, f32[4]{0:T(128)S(1)} %get-tuple-element.12, f32[4]{0:T(128)S(1)} %get-tuple-element.13, f32[4]{0:T(128)S(1)} %get-tuple-element.14, f32[4]{0:T(128)S(1)} %get-tuple-element.15, ...), kind=kLoop, calls=%fused_computation.140 | loop fusion | flops 35651584 | bytes 83886224 | tf_op jit(solution)/shard_map/add | solution.py:70
  1908.0 41.6 %fusion.133 = f32[32,64,256]{2,0,1:T(8,128)} fusion(f32[4,32,64,256]{3,1,2,0:T(8,128)} %fusion.83, f32[4]{0:T(128)S(1)} %get-tuple-element.3, f32[4]{0:T(128)S(1)} %get-tuple-element.4, f32[4]{0:T(128)S(1)} %get-tuple-element.5, f32[4]{0:T(128)S(1)} %get-tuple-element.6, f32[4]{0:T(128)S(1)} %get-tuple-element.7, f32[4]{0:T(128)S(1)} %get-tuple-element.8, ...), kind=kLoop, calls=%fused_computation.229 | loop fusion | flops 37224448 | bytes 10485904 | tf_op jit(solution)/shard_map/reduce_sum | solution.py:132
  (143 shorter events, 504.5 us)
Async XLA Ops:
  41.6 35.8 %copy-start = (f32[256,32,256]{2,0,1:T(8,128)}, f32[256,32,256]{2,0,1:T(8,128)S(1)}, u32[]{:S(2)}) copy-start(f32[256,32,256]{2,0,1:T(8,128)S(1)} %fusion.129) | copy-start | bytes 25165828
  85.5 188.2 %all-to-all-start = ((f32[32,256,256]{2,0,1:T(8,128)}), f32[32,256,256]{2,0,1:T(8,128)}, u32[]{:S(2)}, u32[]{:S(2)}) async-start(f32[32,256,256]{2,0,1:T(8,128)} %copy.153), calls=%async_computation | async-start | bytes 16777216 | tf_op jit(solution)/shard_map/all_to_all | solution.py:100
  273.7 187.3 %all-to-all-start.1 = ((f32[32,256,256]{2,0,1:T(8,128)}), f32[32,256,256]{2,0,1:T(8,128)}, u32[]{:S(2)}, u32[]{:S(2)}) async-start(f32[32,256,256]{2,0,1:T(8,128)} %copy.160), calls=%async_computation.1 | async-start | bytes 16777216 | tf_op jit(solution)/shard_map/all_to_all | solution.py:101
  278.7 549.7 %all-reduce.7.cloned.1.call-start = ((), (), s32[]{:S(2)}) async-start(), calls=%async_computation.5 | async-start | bytes 33554432 | tf_op jit(solution)/shard_map/psum | solution.py:109
  864.6 187.8 %all-to-all-start.3 = ((f32[256,32,256]{2,1,0:T(8,128)}), f32[256,32,256]{2,1,0:T(8,128)}, u32[]{:S(2)}, u32[]{:S(2)}) async-start(f32[256,32,256]{2,1,0:T(8,128)} %copy.173), calls=%async_computation.3 | async-start | bytes 16777216 | tf_op jit(solution)/shard_map/all_to_all | solution.py:114
  1052.4 187.2 %all-to-all-start.2 = ((f32[256,32,256]{2,1,0:T(8,128)}), f32[256,32,256]{2,1,0:T(8,128)}, u32[]{:S(2)}, u32[]{:S(2)}) async-start(f32[256,32,256]{2,1,0:T(8,128)} %copy.168), calls=%async_computation.2 | async-start | bytes 16777216 | tf_op jit(solution)/shard_map/all_to_all | solution.py:113
  1239.6 144.5 %all-to-all-start.4 = ((f32[1,32,256,256]{3,1,0,2:T(8,128)}), f32[1,32,256,256]{3,1,0,2:T(8,128)}, u32[]{:S(2)}, u32[]{:S(2)}) async-start(f32[1,32,256,256]{3,1,0,2:T(8,128)} %copy.178), calls=%async_computation.4 | async-start | bytes 16777216 | tf_op jit(solution)/shard_map/all_to_all | solution.py:121
  1297.7 48.1 %copy-start.12 = (f32[4,3,9]{2,0,1:T(4,128)S(1)}, f32[4,3,9]{2,0,1:T(4,128)}, u32[]{:S(2)}) copy-start(f32[4,3,9]{2,0,1:T(4,128)} %param.5) | copy-start | bytes 1300
  1302.0 35.8 %collective-permute-start = (f32[32,4,256]{2,1,0:T(4,128)S(1)}, f32[32,4,256]{2,1,0:T(4,128)S(1)}, u32[]{:S(2)}, u32[]{:S(2)}) collective-permute-start(f32[32,4,256]{2,1,0:T(4,128)S(1)} %get-tuple-element.69), channel_id=1, source_target_pairs={{0,8},{8,16},{16,24},{1,9},{9,17},{17,25},{2,10},{10,18},{18,26},{... | collective-permute-start | bytes 393224 | tf_op jit(solution)/shard_map/ppermute | solution.py:21
  1305.5 34.0 %collective-permute-start.1 = (f32[32,4,256]{2,1,0:T(4,128)S(1)}, f32[32,4,256]{2,1,0:T(4,128)S(1)}, u32[]{:S(2)}, u32[]{:S(2)}) collective-permute-start(f32[32,4,256]{2,1,0:T(4,128)S(1)} %get-tuple-element.70), channel_id=1, source_target_pairs={{8,0},{16,8},{24,16},{9,1},{17,9},{25,17},{10,2},{18,10},{26,18},{... | collective-permute-start | bytes 393224 | tf_op jit(solution)/shard_map/ppermute | solution.py:22
  1339.6 8.5 collective-permute-start.2
  1341.8 9.3 collective-permute-start.3
  1430.4 9.9 collective-permute-start.4
  1434.2 10.5 collective-permute-start.5
  1456.4 24.4 %collective-permute-start.6 = (f32[4,4,72,256]{3,1,2,0:T(4,128)S(1)}, f32[4,4,72,256]{3,1,2,0:T(4,128)S(1)}, u32[]{:S(2)}, u32[]{:S(2)}) collective-permute-start(f32[4,4,72,256]{3,1,2,0:T(4,128)S(1)} %get-tuple-element.39), channel_id=1, source_target_pairs={{0,1},{1,2},{2,3},{3,4},{4,5},{5,6},{6,7},{8,9},{9,10},{10,11},{11... | collective-permute-start | bytes 3538952 | tf_op jit(solution)/shard_map/ppermute | solution.py:21
  1458.3 47.8 %collective-permute-start.7 = (f32[4,4,72,256]{3,1,2,0:T(4,128)S(1)}, f32[4,4,72,256]{3,1,2,0:T(4,128)S(1)}, u32[]{:S(2)}, u32[]{:S(2)}) collective-permute-start(f32[4,4,72,256]{3,1,2,0:T(4,128)S(1)} %get-tuple-element.40), channel_id=1, source_target_pairs={{1,0},{2,1},{3,2},{4,3},{5,4},{6,5},{7,6},{9,8},{10,9},{11,10},{12... | collective-permute-start | bytes 3538952 | tf_op jit(solution)/shard_map/ppermute | solution.py:22
  1640.0 4.3 collective-permute-start.8
  1641.9 6.3 collective-permute-start.9
  1648.3 9.5 collective-permute-start.10
  1650.2 14.0 collective-permute-start.11
  1746.4 8.0 collective-permute-start.12
  1748.4 10.5 collective-permute-start.13
  1770.6 24.9 %collective-permute-start.14 = (f32[4,4,72,256]{3,1,2,0:T(4,128)S(1)}, f32[4,4,72,256]{3,1,2,0:T(4,128)S(1)}, u32[]{:S(2)}, u32[]{:S(2)}) collective-permute-start(f32[4,4,72,256]{3,1,2,0:T(4,128)S(1)} %get-tuple-element.35), channel_id=1, source_target_pairs={{0,1},{1,2},{2,3},{3,4},{4,5},{5,6},{6,7},{8,9},{9,10},{10,11},{11... | collective-permute-start | bytes 3538952 | tf_op jit(solution)/shard_map/ppermute | solution.py:21
  1772.5 48.3 %collective-permute-start.15 = (f32[4,4,72,256]{3,1,2,0:T(4,128)S(1)}, f32[4,4,72,256]{3,1,2,0:T(4,128)S(1)}, u32[]{:S(2)}, u32[]{:S(2)}) collective-permute-start(f32[4,4,72,256]{3,1,2,0:T(4,128)S(1)} %get-tuple-element.36), channel_id=1, source_target_pairs={{1,0},{2,1},{3,2},{4,3},{5,4},{6,5},{7,6},{9,8},{10,9},{11,10},{12... | collective-permute-start | bytes 3538952 | tf_op jit(solution)/shard_map/ppermute | solution.py:22
  (17 other events, 216.2 us)
Sparse Core Ops, SparseCore 0:
  540.3 288.0 all-reduce.6
where the time goes:
time: 1970 us; the launch traced here: 1960 us
  waiting for transfers between devices  1040 us (53%)
  other arithmetic  415 us (21%)
  matrix products  298 us (15%)
  local copies, waits for them, and re-layouts  118 us (6%)
  starting transfers between devices  71.9 us (4%)
    dot_general x20, matrix products, mix(): return jnp.einsum(form, left, right, precision=lax.Precision.HIGHEST)  298 us
    psum x1, waiting for transfers between devices, body(): summed_real, summed_imag = lax.psum((weighted_real, weighted_imag), 'view')  288 us
    add x8, other arithmetic, valid_conv(): running + column[offset] * lax.slice_in_dim(padded, offset, offset + leng...  176 us
    all_to_all x1, waiting for transfers between devices, body(): lax.all_to_all(second_imag, 'pencil', split_axis=1, concat_axis=0, tiled=...  174 us
    all_to_all x1, waiting for transfers between devices, body(): lax.all_to_all(inv_imag, 'pencil', split_axis=0, concat_axis=1, tiled=True)  150 us
    all_to_all x1, waiting for transfers between devices, body(): lax.all_to_all(inv_real, 'pencil', split_axis=0, concat_axis=1, tiled=True)  143 us
    all_to_all x1, waiting for transfers between devices, body(): lax.all_to_all(second_real, 'pencil', split_axis=1, concat_axis=0, tiled=...  135 us
    div x2, other arithmetic, body(): ratio = stacked / blurred  90.1 us
  transfers between devices with their start and end apart: 22, of which 20 were waited for; matrix products, arithmetic and copies ran while one was open for 11% of the time, Pallas kernels for 0%

commit v1 on v0

v1 whole, which is shorter than its diff:
```python
import math

import jax
import jax.numpy as jnp
from jax import lax
from jax.sharding import PartitionSpec as P

ITERS = 2
CHUNKS = 2


def padded_2(shard, sides, width):
    for axis, dim in sides:
        devices, length = (lax.axis_size(axis), shard.shape[dim])
        up = [(i, (i + 1) % devices) for i in range(devices - 1)]
        down = [(j, i) for i, j in up]
        last = lax.slice_in_dim(shard, length - width, length, axis=dim)
        leading = lax.slice_in_dim(shard, 0, width, axis=dim)
        before = lax.ppermute(last, axis, up)
        after = lax.ppermute(leading, axis, down)
        shard = jnp.concatenate([before, shard, after], axis=dim)
    return shard


def tables(length):
    positions = jnp.arange(length, dtype=jnp.int32)
    product = positions[:, None] * positions[None, :] % length
    phases = product.astype(jnp.float32) * (2.0 * math.pi / length)
    return (jnp.cos(phases), jnp.sin(phases))


def mix(form, left, right):
    return jnp.einsum(form, left, right, precision=lax.Precision.HIGH)


def folded(full, axis, dim, width):
    devices, length = (lax.axis_size(axis), full.shape[dim] - 2 * width)
    up = [(i, (i + 1) % devices) for i in range(devices - 1)]
    down = [(j, i) for i, j in up]
    before = lax.slice_in_dim(full, 0, width, axis=dim)
    after = lax.slice_in_dim(full, length + width, length + 2 * width, axis=dim)
    own = lax.slice_in_dim(full, width, length + width, axis=dim)
    from_below = lax.ppermute(after, axis, up)
    from_above = lax.ppermute(before, axis, down)
    spread = [(0, 0, 0)] * full.ndim
    spread[dim] = (0, length - width, 0)
    lower = lax.pad(from_below, jnp.float32(0), spread)
    spread[dim] = (length - width, 0, 0)
    return own + lower + lax.pad(from_above, jnp.float32(0), spread)


def band(taps, rows, columns, shift):
    offset = jnp.arange(columns)[None, :] - jnp.arange(rows)[:, None] + shift
    total = jnp.zeros((taps.shape[0], rows, columns), jnp.float32)
    for t in range(taps.shape[1]):
        total = total + jnp.where(offset == t, taps[:, t, None, None], 0.0)
    return total


def joined_of(slab, weights):
    view_count, view_index = lax.axis_size("view"), lax.axis_index("view")
    nx, ny = slab.shape[2], slab.shape[1]
    cos_x, sin_x = tables(nx)
    cos_y, sin_y = tables(ny)
    width = nx // CHUNKS
    sent = []
    for chunk in range(CHUNKS):
        part = slice(chunk * width, (chunk + 1) * width)
        real = mix("zyx,xk->zyk", slab, cos_x[:, part])
        imag = -mix("zyx,xk->zyk", slab, sin_x[:, part])
        out_real = mix("zyx,yk->zkx", real, cos_y) + mix("zyx,yk->zkx", imag, sin_y)
        out_imag = mix("zyx,yk->zkx", imag, cos_y) - mix("zyx,yk->zkx", real, sin_y)
        sent.append([
            lax.all_to_all(piece, "pencil", split_axis=1, concat_axis=0, tiled=True)
            for piece in (out_real, out_imag)
        ])
    inverse = []
    for chunk in range(CHUNKS):
        real, imag = sent[chunk]
        nz = real.shape[0]
        cos_z, sin_z = tables(nz)
        weight = weights[:, :, chunk * width:(chunk + 1) * width]
        out_real = weight * (mix("zyx,zk->kyx", real, cos_z) + mix("zyx,zk->kyx", imag, sin_z))
        out_imag = weight * (mix("zyx,zk->kyx", imag, cos_z) - mix("zyx,zk->kyx", real, sin_z))
        real = lax.psum_scatter(out_real, "view", scatter_dimension=1, tiled=True)
        imag = lax.psum_scatter(out_imag, "view", scatter_dimension=1, tiled=True)
        inverse.append((
            mix("kyx,kz->zyx", real, cos_z) - mix("kyx,kz->zyx", imag, sin_z),
            mix("kyx,kz->zyx", real, sin_z) + mix("kyx,kz->zyx", imag, cos_z),
        ))
    real = jnp.concatenate([pair[0] for pair in inverse], axis=2)
    imag = jnp.concatenate([pair[1] for pair in inverse], axis=2)
    rows = real.shape[1]
    moved = [
        lax.all_to_all(piece, "pencil", split_axis=0, concat_axis=1, tiled=True)
        for piece in (
            mix("zyk,kx->zyx", real, cos_x) - mix("zyk,kx->zyx", imag, sin_x),
            mix("zyk,kx->zyx", real, sin_x) + mix("zyk,kx->zyx", imag, cos_x),
        )
    ]
    scale = 1.0 / float(nz * ny * nx)
    held = [
        lax.dynamic_index_in_dim(
            table.reshape(-1, view_count, rows, ny), view_index, 1, keepdims=False
        ).reshape(-1, ny) * scale
        for table in (cos_y, sin_y)
    ]
    partial = mix("zkx,ky->zyx", moved[0], held[0]) - mix("zkx,ky->zyx", moved[1], held[1])
    return lax.psum_scatter(partial, "view", scatter_dimension=1, tiled=True)


def body(recorded, spectral_weight, psf_taps):
    view_count = lax.axis_size("view")
    joined_volume = joined_of(recorded[0], spectral_weight[0])
    kernels = psf_taps / jnp.sum(psf_taps, axis=-1, keepdims=True)
    margin = kernels.shape[-1] // 2
    stacked = lax.all_to_all(recorded, "view", split_axis=2, concat_axis=0, tiled=True)
    depth, rows, length = joined_volume.shape
    views = kernels.shape[0]
    blur_z = band(kernels[:, 0], depth, depth + 2 * margin, 0)
    blur_y = band(kernels[:, 1], rows, rows + 2 * margin, 0)
    blur_x = band(kernels[:, 2], length, length, margin)
    local = 0.1 + jax.nn.softplus(joined_volume)
    for repeat in range(ITERS):
        padded = padded_2(local, (("view", 1), ("pencil", 0)), margin)
        field = mix("vza,abx->vzbx", blur_z, padded)
        field = mix("vyb,vzbx->vzyx", blur_y, field)
        ratio = stacked / mix("vzyx,vcx->vzyc", field, blur_x)
        field = mix("vzyc,vcx->vzyx", ratio, blur_x)
        field = mix("vyb,vzyx->vzbx", blur_y, field)
        total = mix("vza,vzbx->abx", blur_z, field)
        total = folded(folded(total, "pencil", 0, margin), "view", 1, margin)
        local = local * total / view_count
    return (joined_volume, local)


def solution(mesh):
    return jax.shard_map(
        body,
        mesh=mesh,
        in_specs=(P("view", "pencil", None, None), P("view", None, "pencil", None), P()),
        out_specs=(P("pencil", "view", None), P("pencil", "view", None)),
        check_vma=False,
    )
```

time: 1970 us -> 1060 us (0.54)
  waiting for transfers between devices: 1040 us -> 580 us
  other arithmetic: 415 us -> 20 us
  matrix products: 298 us -> 259 us
  local copies, waits for them, and re-layouts: 118 us -> 95 us
    psum x1 -> x0, waiting for transfers between devices: 288 us -> none  [body(): summed_real, summed_imag = lax.psum((weighted_real, weighted_imag), 'view')]
    all_to_all x4 -> x6, waiting for transfers between devices: 601 us -> 362 us  [the longest x4 283 us: joined_of(): lax.all_to_all(piece, 'pencil', split_axis=1, concat_axis=0, tiled=True)]
    add x8 -> x4, other arithmetic: 176 us -> 3.05 us  [the longest x2 2.77 us: folded(): return own + lower + lax.pad(from_above, jnp.float32(0), spread)]
    reduce_scatter x0 -> x5, waiting for transfers between devices: none -> 148 us  [the longest x1 91 us: joined_of(): return lax.psum_scatter(partial, 'view', scatter_dimension=1, tiled=True)]
    div x4 -> x2, other arithmetic: 98.6 us -> 3.38 us  [body(): local = local * total / view_count]
    reduce_sum x2 -> x1, other arithmetic: 84 us -> 0.09 us  [body(): kernels = psf_taps / jnp.sum(psf_taps, axis=-1, keepdims=True)]
    ppermute x8 -> x4, waiting for transfers between devices: 74.7 us -> 12.1 us  [padded_2(): after = lax.ppermute(leading, axis, down)]
    dot_general x20 -> x38, matrix products: 298 us -> 240 us  [mix(): return jnp.einsum(form, left, right, precision=lax.Precision.HIGH)]
  transfers between devices with their start and end apart: 22 -> 28, of which waited for: 20 -> 20; matrix products, arithmetic and copies ran while one was open for 11% -> 19% of each run, Pallas kernels for 0% -> 0%
where the time goes in v1:
time: 1060 us; the launch traced here: 1050 us
  waiting for transfers between devices  580 us (55%)
  matrix products  259 us (24%)
  local copies, waits for them, and re-layouts  95 us (9%)
  starting transfers between devices  80.9 us (8%)
  other arithmetic  20 us (2%)
  between operations  16.2 us (2%)
    all_to_all x4, waiting for transfers between devices, joined_of(): lax.all_to_all(piece, 'pencil', split_axis=1, concat_axis=0, tiled=True)  283 us
    dot_general x38, matrix products, mix(): return jnp.einsum(form, left, right, precision=lax.Precision.HIGH)  240 us
    reduce_scatter x1, waiting for transfers between devices, joined_of(): return lax.psum_scatter(partial, 'view', scatter_dimension=1, tiled=True)  91 us
    all_to_all x2, waiting for transfers between devices, joined_of(): lax.all_to_all(piece, 'pencil', split_axis=0, concat_axis=1, tiled=True)  79 us
    ppermute x4, waiting for transfers between devices, padded_2(): before = lax.ppermute(last, axis, up)  34 us
    unnamed x188, local copies, waits for them, and re-layouts  33.9 us
    reduce_scatter x2, waiting for transfers between devices, joined_of(): real = lax.psum_scatter(out_real, 'view', scatter_dimension=1, tiled=True)  30.1 us
    reduce_scatter x2, waiting for transfers between devices, joined_of(): imag = lax.psum_scatter(out_imag, 'view', scatter_dimension=1, tiled=True)  27.2 us
  transfers between devices with their start and end apart: 28, of which 20 were waited for; matrix products, arithmetic and copies ran while one was open for 19% of the time, Pallas kernels for 0%

profile of v1, /device:TPU:25, one launch (start us, length us, event | category | flops | bytes accessed | tf_op | source)
XLA Modules:
  0.0 1051.3 jit_solution(16029238604463743606)
XLA Ops:
  9.1 8.0 fusion.12
  53.4 79.3 %all-to-all-done = f32[32,256,128]{2,0,1:T(8,128)} async-done(((f32[32,256,128]{2,0,1:T(8,128)}), f32[32,256,128]{2,0,1:T(8,128)}, u32[]{:S(2)}, u32[]{:S(2)}) %all-to-all-start) | async-done | bytes 4194336 | tf_op jit(solution)/shard_map/all_to_all | solution.py:74
  137.8 11.7 %copy.275 = f32[1,256,32,256]{3,1,2,0:T(8,128)} copy(f32[1,256,32,256]{3,2,1,0:T(8,128)} %param.4) | data formatting | bytes 16777216 | tf_op args[1]
  179.4 50.5 %all-to-all-done.1 = f32[32,256,128]{2,0,1:T(8,128)} async-done(((f32[32,256,128]{2,0,1:T(8,128)}), f32[32,256,128]{2,0,1:T(8,128)}, u32[]{:S(2)}, u32[]{:S(2)}) %all-to-all-start.1) | async-done | bytes 4194336 | tf_op jit(solution)/shard_map/all_to_all | solution.py:74
  242.5 8.6 subtract_bitcast_fusion.1
  278.4 74.2 %all-to-all-done.3 = f32[32,256,128]{2,0,1:T(8,128)} async-done(((f32[32,256,128]{2,0,1:T(8,128)}), f32[32,256,128]{2,0,1:T(8,128)}, u32[]{:S(2)}, u32[]{:S(2)}) %all-to-all-start.3) | async-done | bytes 4194336 | tf_op jit(solution)/shard_map/all_to_all | solution.py:74
  357.3 9.0 subtract_multiply_fusion.1
  371.2 78.6 %all-to-all-done.2 = f32[32,256,128]{2,0,1:T(8,128)} async-done(((f32[32,256,128]{2,0,1:T(8,128)}), f32[32,256,128]{2,0,1:T(8,128)}, u32[]{:S(2)}, u32[]{:S(2)}) %all-to-all-start.2) | async-done | bytes 4194336 | tf_op jit(solution)/shard_map/all_to_all | solution.py:74
  468.8 8.5 add_multiply_fusion
  480.5 27.2 %reduce-scatter.12.cloned.1.call-done = f32[256,8,128]{2,0,1:T(8,128)} async-done(((f32[256,32,128]{2,0,1:T(8,128)}), f32[256,8,128]{2,0,1:T(8,128)}) %reduce-scatter.12.cloned.1.call-update) | async-done | bytes 1048592 | tf_op jit(solution)/shard_map/reduce_scatter | solution.py:86
  524.6 30.1 %reduce-scatter.10.cloned.1.call-done = f32[256,8,128]{2,0,1:T(8,128)} async-done(((f32[256,32,128]{2,0,1:T(8,128)}), f32[256,8,128]{2,0,1:T(8,128)}) %reduce-scatter.10.cloned.1.call-update) | async-done | bytes 1048592 | tf_op jit(solution)/shard_map/reduce_scatter | solution.py:85
  582.3 39.7 %all-to-all-done.4 = f32[256,8,256]{2,1,0:T(8,128)} async-done(((f32[256,8,256]{2,1,0:T(8,128)}), f32[256,8,256]{2,1,0:T(8,128)}, u32[]{:S(2)}, u32[]{:S(2)}) %all-to-all-start.4) | async-done | bytes 2097184 | tf_op jit(solution)/shard_map/all_to_all | solution.py:95
  634.9 39.3 %all-to-all-done.5 = f32[256,8,256]{2,1,0:T(8,128)S(1)} async-done(((f32[256,8,256]{2,1,0:T(8,128)}), f32[256,8,256]{2,1,0:T(8,128)S(1)}, u32[]{:S(2)}, u32[]{:S(2)}) %all-to-all-start.5) | async-done | bytes 2097184 | tf_op jit(solution)/shard_map/all_to_all | solution.py:95
  674.1 8.5 subtract_bitcast_fusion
  682.6 13.5 %copy.158 = f32[1,32,256,256]{3,1,0,2:T(8,128)} copy(f32[1,32,256,256]{3,2,1,0:T(8,128)} %param.3) | data formatting | bytes 16777216 | tf_op args[0]
  707.1 91.0 %reduce-scatter.14.cloned.1.call-done = f32[32,64,256]{2,1,0:T(8,128)} async-done(((f32[32,256,256]{2,1,0:T(8,128)}), f32[32,64,256]{2,1,0:T(8,128)}) %reduce-scatter.14.cloned.1.call-update) | async-done | bytes 2097168 | tf_op jit(solution)/shard_map/reduce_scatter | solution.py:109
  808.5 30.7 %collective-permute-done = f32[32,4,256]{2,1,0:T(4,128)S(1)} collective-permute-done((f32[32,4,256]{2,1,0:T(4,128)S(1)}, f32[32,4,256]{2,1,0:T(4,128)S(1)}, u32[]{:S(2)}, u32[]{:S(2)}) %collective-permute-start) | collective-permute-done | bytes 131104 | tf_op jit(solution)/shard_map/ppermute | solution.py:19
  852.5 11.5 %copy.159 = f32[1,32,256,256]{3,2,1,0:T(8,128)} copy(f32[1,32,256,256]{3,1,0,2:T(8,128)} %all-to-all-done.6) | data formatting | bytes 16777216 | tf_op jit(solution)/shard_map/all_to_all | solution.py:117
  870.2 10.8 %fusion.44 = f32[4,32,64,256]{3,2,1,0:T(8,128)} fusion(f32[4,32,72,256]{3,1,2,0:T(8,128)S(1)} %fusion.52, f32[4]{0:T(128)S(1)} %copy-done.66, f32[4]{0:T(128)S(1)} %copy-done.67, f32[4]{0:T(128)S(1)} %copy-done.68, f32[4]{0:T(128)S(1)} %copy-done.69, f32[4]{0:T(128)S(1)} %copy-done.70, f32[4]{0:T(128)S(1)} %copy-done.71, f32[4]{0:T(128)S(1)} %copy-done.72, ...), kind=kOutput, calls=%fused_computation.57 | convolution fusion | flops 906283008 | bytes 17867408 | tf_op jit(solution)/shard_map/vyb,vzbx->vzyx/dot_general | solution.py:33
  881.1 12.1 %fusion.56 = f32[4,32,64,256]{3,2,0,1:T(8,128)} fusion(f32[4,32,64,256]{3,2,0,1:T(8,128)S(1)} %bitcast.273, f32[4,32,64,256]{3,2,1,0:T(8,128)} %fusion.44, f32[4]{0:T(128)S(1)} %copy-done.75, f32[4]{0:T(128)S(1)} %copy-done.76, f32[4]{0:T(128)S(1)} %copy-done.77, f32[4]{0:T(128)S(1)} %copy-done.78, f32[4]{0:T(128)S(1)} %copy-done.79, f32[4]{0:T(128)S(1)} %copy-done.80, ...), kind=kOutput, calls=%fused_computation.67 | convolution fusion | flops 3227779072 | bytes 25755792 | tf_op jit(solution)/shard_map/vzyx,vcx->vzyc/dot_general | solution.py:33
  893.2 8.2 fusion.20
  965.9 10.7 %fusion.47 = f32[4,32,64,256]{3,2,1,0:T(8,128)} fusion(f32[4,32,72,256]{3,1,2,0:T(8,128)S(1)} %fusion.50, f32[4]{0:T(128)S(1)} %copy-done.66, f32[4]{0:T(128)S(1)} %copy-done.67, f32[4]{0:T(128)S(1)} %copy-done.68, f32[4]{0:T(128)S(1)} %copy-done.69, f32[4]{0:T(128)S(1)} %copy-done.70, f32[4]{0:T(128)S(1)} %copy-done.71, f32[4]{0:T(128)S(1)} %copy-done.72, ...), kind=kOutput, calls=%fused_computation.58 | convolution fusion | flops 906283008 | bytes 17867408 | tf_op jit(solution)/shard_map/vyb,vzbx->vzyx/dot_general | solution.py:33
  976.7 13.9 %fusion.59 = f32[4,32,64,256]{3,2,0,1:T(8,128)} fusion(f32[4,32,64,256]{3,2,0,1:T(8,128)} %bitcast.270, f32[4,32,64,256]{3,2,1,0:T(8,128)} %fusion.47, f32[4]{0:T(128)S(1)} %copy-done.75, f32[4]{0:T(128)S(1)} %copy-done.76, f32[4]{0:T(128)S(1)} %copy-done.77, f32[4]{0:T(128)S(1)} %copy-done.78, f32[4]{0:T(128)S(1)} %copy-done.79, f32[4]{0:T(128)S(1)} %copy-done.80, ...), kind=kOutput, calls=%fused_computation.68 | convolution fusion | flops 3227779072 | bytes 25755792 | tf_op jit(solution)/shard_map/vzyx,vcx->vzyc/dot_general | solution.py:33
  990.6 11.2 %fusion.16 = f32[4,32,64,256]{3,2,1,0:T(8,128)} fusion(f32[4,32,64,256]{3,2,0,1:T(8,128)} %fusion.59, f32[4]{0:T(128)S(1)} %copy-done.75, f32[4]{0:T(128)S(1)} %copy-done.76, f32[4]{0:T(128)S(1)} %copy-done.77, f32[4]{0:T(128)S(1)} %copy-done.78, f32[4]{0:T(128)S(1)} %copy-done.79, f32[4]{0:T(128)S(1)} %copy-done.80, f32[4]{0:T(128)S(1)} %copy-done.81, ...), kind=kOutput, calls=%fused_computation.16 | convolution fusion | flops 3225681920 | bytes 17367184 | tf_op jit(solution)/shard_map/vzyc,vcx->vzyx/dot_general | solution.py:33
  (348 shorter events, 348.3 us)
Async XLA Ops:
  34.8 98.0 %all-to-all-start = ((f32[32,256,128]{2,0,1:T(8,128)}), f32[32,256,128]{2,0,1:T(8,128)}, u32[]{:S(2)}, u32[]{:S(2)}) async-start(f32[32,256,128]{2,0,1:T(8,128)} %copy.116), calls=%async_computation | async-start | bytes 8388608 | tf_op jit(solution)/shard_map/all_to_all | solution.py:74
  132.8 97.1 %all-to-all-start.1 = ((f32[32,256,128]{2,0,1:T(8,128)}), f32[32,256,128]{2,0,1:T(8,128)}, u32[]{:S(2)}, u32[]{:S(2)}) async-start(f32[32,256,128]{2,0,1:T(8,128)} %copy.120), calls=%async_computation.1 | async-start | bytes 8388608 | tf_op jit(solution)/shard_map/all_to_all | solution.py:74
  137.4 339.9 %reduce-scatter.6.cloned.1.call-start = ((), (), s32[]{:S(2)}) async-start(), calls=%async_computation.12 | async-start | bytes 5242880 | tf_op jit(solution)/shard_map/reduce_scatter | solution.py:85
  255.6 97.1 %all-to-all-start.3 = ((f32[32,256,128]{2,0,1:T(8,128)}), f32[32,256,128]{2,0,1:T(8,128)}, u32[]{:S(2)}, u32[]{:S(2)}) async-start(f32[32,256,128]{2,0,1:T(8,128)} %copy.132), calls=%async_computation.5 | async-start | bytes 8388608 | tf_op jit(solution)/shard_map/all_to_all | solution.py:74
  352.7 97.1 %all-to-all-start.2 = ((f32[32,256,128]{2,0,1:T(8,128)}), f32[32,256,128]{2,0,1:T(8,128)}, u32[]{:S(2)}, u32[]{:S(2)}) async-start(f32[32,256,128]{2,0,1:T(8,128)} %copy.128), calls=%async_computation.4 | async-start | bytes 8388608 | tf_op jit(solution)/shard_map/all_to_all | solution.py:74
  357.3 121.6 %reduce-scatter.8.cloned.1.call-start = ((), (), s32[]{:S(2)}) async-start(), calls=%async_computation.13 | async-start | bytes 5242880 | tf_op jit(solution)/shard_map/reduce_scatter | solution.py:86
  366.4 141.3 %reduce-scatter.12.cloned.1.call-start = ((), (), s32[]{:S(2)}) async-start(), calls=%async_computation.15 | async-start | bytes 5242880 | tf_op jit(solution)/shard_map/reduce_scatter | solution.py:86
  463.2 91.5 %reduce-scatter.10.cloned.1.call-start = ((), (), s32[]{:S(2)}) async-start(), calls=%async_computation.14 | async-start | bytes 5242880 | tf_op jit(solution)/shard_map/reduce_scatter | solution.py:85
  569.1 53.0 %all-to-all-start.4 = ((f32[256,8,256]{2,1,0:T(8,128)}), f32[256,8,256]{2,1,0:T(8,128)}, u32[]{:S(2)}, u32[]{:S(2)}) async-start(f32[256,8,256]{2,1,0:T(8,128)} %copy.150), calls=%async_computation.8 | async-start | bytes 4194304 | tf_op jit(solution)/shard_map/all_to_all | solution.py:95
  622.1 52.1 %all-to-all-start.5 = ((f32[256,8,256]{2,1,0:T(8,128)}), f32[256,8,256]{2,1,0:T(8,128)S(1)}, u32[]{:S(2)}, u32[]{:S(2)}) async-start(f32[256,8,256]{2,1,0:T(8,128)} %copy.156), calls=%async_computation.9 | async-start | bytes 4194304 | tf_op jit(solution)/shard_map/all_to_all | solution.py:95
  626.7 171.4 %reduce-scatter.14.cloned.1.call-start = ((), (), s32[]{:S(2)}) async-start(), calls=%async_computation.16 | async-start | bytes 10485760 | tf_op jit(solution)/shard_map/reduce_scatter | solution.py:109
  696.1 156.4 %all-to-all-start.6 = ((f32[1,32,256,256]{3,1,0,2:T(8,128)}), f32[1,32,256,256]{3,1,0,2:T(8,128)}, u32[]{:S(2)}, u32[]{:S(2)}) async-start(f32[1,32,256,256]{3,1,0,2:T(8,128)} %copy.158), calls=%async_computation.11 | async-start | bytes 16777216 | tf_op jit(solution)/shard_map/all_to_all | solution.py:117
  800.9 38.3 %collective-permute-start = (f32[32,4,256]{2,1,0:T(4,128)S(1)}, f32[32,4,256]{2,1,0:T(4,128)S(1)}, u32[]{:S(2)}, u32[]{:S(2)}) collective-permute-start(f32[32,4,256]{2,1,0:T(4,128)S(1)} %get-tuple-element.43), channel_id=1, source_target_pairs={{0,8},{8,16},{16,24},{1,9},{9,17},{17,25},{2,10},{10,18},{18,26},{... | collective-permute-start | bytes 393224 | tf_op jit(solution)/shard_map/ppermute | solution.py:19
  803.6 37.4 %collective-permute-start.1 = (f32[32,4,256]{2,1,0:T(4,128)S(1)}, f32[32,4,256]{2,1,0:T(4,128)S(1)}, u32[]{:S(2)}, u32[]{:S(2)}) collective-permute-start(f32[32,4,256]{2,1,0:T(4,128)S(1)} %get-tuple-element.44), channel_id=1, source_target_pairs={{8,0},{16,8},{24,16},{9,1},{17,9},{25,17},{10,2},{18,10},{26,18},{... | collective-permute-start | bytes 393224 | tf_op jit(solution)/shard_map/ppermute | solution.py:20
  841.8 22.4 %collective-permute-start.2 = (f32[4,72,256]{2,1,0:T(8,128)}, f32[4,72,256]{2,1,0:T(8,128)S(1)}, u32[]{:S(2)}, u32[]{:S(2)}) collective-permute-start(f32[4,72,256]{2,1,0:T(8,128)} %get-tuple-element.39), channel_id=1, source_target_pairs={{0,1},{1,2},{2,3},{3,4},{4,5},{5,6},{6,7},{8,9},{9,10},{10,11},{11... | collective-permute-start | bytes 884744 | tf_op jit(solution)/shard_map/ppermute | solution.py:19
  844.2 20.0 %collective-permute-start.3 = (f32[4,72,256]{2,1,0:T(8,128)S(1)}, f32[4,72,256]{2,1,0:T(8,128)}, u32[]{:S(2)}, u32[]{:S(2)}) collective-permute-start(f32[4,72,256]{2,1,0:T(8,128)S(1)} %get-tuple-element.40), channel_id=1, source_target_pairs={{1,0},{2,1},{3,2},{4,3},{5,4},{6,5},{7,6},{9,8},{10,9},{11,10},{12... | collective-permute-start | bytes 884744 | tf_op jit(solution)/shard_map/ppermute | solution.py:20
  912.2 8.5 collective-permute-start.4
  914.5 9.2 collective-permute-start.5
  929.5 6.3 collective-permute-start.7
  939.3 6.3 collective-permute-start.9
  945.6 9.5 collective-permute-start.10
  947.6 14.0 %collective-permute-start.11 = (f32[4,72,256]{2,1,0:T(8,128)S(1)}, f32[4,72,256]{2,1,0:T(8,128)S(1)}, u32[]{:S(2)}, u32[]{:S(2)}) collective-permute-start(f32[4,72,256]{2,1,0:T(8,128)S(1)} %get-tuple-element.36), channel_id=1, source_target_pairs={{1,0},{2,1},{3,2},{4,3},{5,4},{6,5},{7,6},{9,8},{10,9},{11,10},{12... | collective-permute-start | bytes 884744 | tf_op jit(solution)/shard_map/ppermute | solution.py:20
  1014.8 11.0 %collective-permute-start.12 = (f32[4,72,256]{2,1,0:T(8,128)S(1)}, f32[4,72,256]{2,1,0:T(8,128)S(1)}, u32[]{:S(2)}, u32[]{:S(2)}) collective-permute-start(f32[4,72,256]{2,1,0:T(8,128)S(1)} %copy.222), channel_id=1, source_target_pairs={{0,1},{1,2},{2,3},{3,4},{4,5},{5,6},{6,7},{8,9},{9,10},{10,11},{11... | collective-permute-start | bytes 884744 | tf_op jit(solution)/shard_map/ppermute | solution.py:43
  1016.8 16.1 %collective-permute-start.13 = (f32[4,72,256]{2,1,0:T(8,128)S(1)}, f32[4,72,256]{2,1,0:T(8,128)S(1)}, u32[]{:S(2)}, u32[]{:S(2)}) collective-permute-start(f32[4,72,256]{2,1,0:T(8,128)S(1)} %copy.223), channel_id=1, source_target_pairs={{1,0},{2,1},{3,2},{4,3},{5,4},{6,5},{7,6},{9,8},{10,9},{11,10},{12... | collective-permute-start | bytes 884744 | tf_op jit(solution)/shard_map/ppermute | solution.py:44
  (95 other events, 563.0 us)
Sparse Core Ops, SparseCore 0:
  242.6 44.3 reduce-scatter.5
  366.5 46.5 reduce-scatter.7
  463.3 44.3 reduce-scatter.11
  510.1 44.5 reduce-scatter.9
  682.7 115.3 reduce-scatter.13
